TPU v7x, 32 devices: a whole 2x2x4 slice. The times are simulated.
32 devices in a mesh: row: 8 (over z, y), col: 4 (over x, core).
Axes of the slice: x: 2, y: 2, z: 4, core: 2. Of those that a mesh axis runs over, the one named last changes fastest.
Arguments:
- spectra: bfloat16 [1024, 16, 128], P(('row', 'col')), may hold values from -4 to 4
- window_flags: int32 [1024, 64], P(('row', 'col')), may hold values 0 or 1
- pair_mask: int32 [1024, 1024], P('row', 'col'), may hold values 0 or 1
- misfit_weight: bfloat16 [16, 1024, 1024], P(None, 'row', 'col'), may hold values from 0.0099487305 to 0.099609375
- observed: bfloat16 [2, 16, 1024, 1024], P(None, None, 'row', 'col'), may hold values from -6 to 6
Outputs:
- grad_first: bfloat16 [1024, 16, 128], P(('row', 'col'))
- grad_second: bfloat16 [4, 256, 16, 128], P('col', 'row')
All inputs are finite; a program needn't handle non-finite values. No bound on the sum of `window_flags` or of `pair_mask` on one device may be relied on, other than what follows from the above.
Results may differ from a plain program's by a relative error of at most 0.019.
Values may be sent and summed in bfloat16 or wider, within the bound.
A program may use at most 64 MiB of HBM per device.

v0:
```python
import jax
import jax.numpy as jnp
from jax import lax
from jax.sharding import PartitionSpec as P


def swap_parts(values, half_width):
    return jnp.concatenate([-values[..., half_width:], values[..., :half_width]], axis=-1)


def per_device(spectra, window_flags, pair_mask, misfit_weight, observed):
    half_width = spectra.shape[2] // 2
    flag_value = window_flags.astype(jnp.bfloat16)
    flag_both = jnp.concatenate([flag_value, flag_value], axis=1)
    flagged = spectra * flag_both[:, None, :]
    first_side = lax.all_gather(flagged, "col", axis=0, tiled=True)
    block_ratio = lax.axis_size("row") // lax.axis_size("col")
    strided = lax.all_gather(flagged, "row", axis=0, tiled=True)
    regrouped = lax.all_to_all(strided, "col", split_axis=0, concat_axis=0, tiled=True)
    col_count = lax.axis_size("col")
    shard_rows = flagged.shape[0]
    regrouped = regrouped.reshape(
        col_count, block_ratio, shard_rows, flagged.shape[1], flagged.shape[2]
    )
    second_side = jnp.transpose(regrouped, (1, 0, 2, 3, 4)).reshape(
        -1, flagged.shape[1], flagged.shape[2]
    )
    col_stack = jnp.stack([second_side, swap_parts(second_side, half_width)])
    row_stack = jnp.stack([first_side, -swap_parts(first_side, half_width)])
    cross_spec = jnp.einsum(
        "ifk,cjfk->cfij", first_side, col_stack, preferred_element_type=jnp.float32
    )
    residual = (
        pair_mask.astype(jnp.float32)[None, None]
        * misfit_weight.astype(jnp.float32)[None]
        * (cross_spec - observed.astype(jnp.float32))
    ).astype(jnp.bfloat16)
    residual_part = residual
    grad_first = lax.psum_scatter(
        jnp.einsum(
            "cfij,cjfk->ifk", residual_part, col_stack, preferred_element_type=jnp.float32
        ).astype(jnp.bfloat16),
        "col",
        scatter_dimension=0,
        tiled=True,
    )
    residual_part = residual
    grad_second = lax.psum_scatter(
        jnp.einsum(
            "cfij,cifk->jfk", residual_part, row_stack, preferred_element_type=jnp.float32
        ).astype(jnp.bfloat16),
        "row",
        scatter_dimension=0,
        tiled=True,
    )
    return (grad_first, grad_second[None])


def solution(mesh):
    placed = (
        P(("row", "col"), None, None),
        P(("row", "col"), None),
        P("row", "col"),
        P(None, "row", "col"),
        P(None, None, "row", "col"),
    )
    return jax.shard_map(
        per_device,
        mesh=mesh,
        in_specs=placed,
        out_specs=(P(("row", "col"), None, None), P("col", "row", None, None)),
        check_vma=False,
    )
```

profile of v0, /device:TPU:0, one launch (start us, length us, event | category | flops | bytes accessed | tf_op | source)
XLA Modules:
  0.0 180.4 jit_solution(5672547921688887537)
XLA Ops:
  7.2 0.0 all-gather.2.cloned.1.call-start
  7.2 0.7 convert_element_type.27
  7.9 0.1 pad_maximum_fusion.7
  8.0 1.6 copy_multiply_fusion
  9.6 0.0 all-gather.2.cloned.1.call-update
  9.6 43.1 %all-gather.2.cloned.1.call-done = bf16[256,16,128]{2,0,1:T(8,128)(2,1)} async-done(((bf16[32,16,128]{2,0,1:T(8,128)(2,1)}), bf16[256,16,128]{2,0,1:T(8,128)(2,1)}) %all-gather.2.cloned.1.call-update) | async-done | bytes 1048592 | tf_op jit(solution)/shard_map/all_gather | solution.py:18
  52.7 2.9 %copy.19 = bf16[256,16,128]{2,1,0:T(8,128)(2,1)} copy(bf16[256,16,128]{2,0,1:T(8,128)(2,1)} %all-gather.2.cloned.1.call-done) | data formatting | bytes 2097152 | tf_op jit(solution)/shard_map/all_gather | solution.py:18
  55.6 4.2 %all-to-all-start = ((bf16[256,16,128]{2,1,0:T(8,128)(2,1)}), bf16[256,16,128]{2,1,0:T(8,128)(2,1)}, u32[]{:S(2)}, u32[]{:S(2)}) async-start(bf16[256,16,128]{2,1,0:T(8,128)(2,1)} %copy.19), calls=%async_computation | async-start | bytes 2097152 | tf_op jit(solution)/shard_map/all_to_all | solution.py:19
  59.9 0.0 reduce-scatter.3.cloned.1.call-start
  60.0 1.6 convert_multiply_fusion
  61.5 1.9 %copy.21 = f32[16,128,256]{1,2,0:T(8,128)S(1)} copy(f32[16,128,256]{2,1,0:T(8,128)} %convert_multiply_fusion) | data formatting | bytes 4194304 | tf_op jit(solution)/shard_map/mul | solution.py:34
  63.4 0.0 copy-start.3
  63.4 4.0 %copy.22 = bf16[2,16,128,256]{2,3,0,1:T(8,128)(2,1)} copy(bf16[2,16,128,256]{3,2,1,0:T(8,128)(2,1)} %param.9) | data formatting | bytes 4194304 | tf_op args[4]
  67.4 10.5 %all_gather.7 = bf16[128,16,128]{2,0,1:T(8,128)(2,1)S(1)} all-gather(bf16[32,16,128]{2,0,1:T(8,128)(2,1)S(1)} %copy-done.3), channel_id=1, replica_groups=mesh['row'=8,'col'=4] {'col'}, dimensions={0}, use_global_device_ids=true | all-gather | bytes 655360 | tf_op jit(solution)/shard_map/all_gather | solution.py:16
  77.9 1.5 copy.20
  79.4 0.4 slice_negate_fusion
  79.9 0.6 maximum_bitcast_fusion
  80.5 1.0 copy-done
  81.5 0.9 fusion.1
  82.4 1.3 copy-done.1
  83.7 0.8 fusion.10
  84.5 1.2 copy.25
  85.7 0.0 reduce-scatter.3.cloned.1.call-update
  85.8 0.0 reduce-scatter.5.cloned.1.call-start
  85.8 0.2 fusion.14
  86.0 0.3 maximum_negate_fusion
  86.4 0.9 copy-done.2
  87.3 1.9 %fusion.6 = bf16[256,16,128]{0,2,1:T(8,128)(2,1)} fusion(bf16[2,16,128,256]{2,3,0,1:T(8,128)(2,1)S(1)} %copy-done.2, bf16[1,128,16,128]{3,1,2,0:T(8,128)(2,1)S(1)} %maximum_negate_fusion, bf16[1,128,16,128]{3,1,2,0:T(8,128)(2,1)S(1)} %bitcast.44), kind=kOutput, calls=%fused_computation.8 | convolution fusion | flops 269484032 | bytes 4194304 | tf_op jit(solution)/shard_map/cfij,cifk->jfk/dot_general | solution.py:49
  89.2 2.6 %copy.28 = bf16[256,16,128]{2,1,0:T(8,128)(2,1)} copy(bf16[256,16,128]{0,2,1:T(8,128)(2,1)} %fusion.6) | data formatting | bytes 2097152 | tf_op jit(solution)/shard_map/convert_element_type | solution.py:51
  91.8 0.0 reduce-scatter.5.cloned.1.call-update
  91.8 13.8 %reduce-scatter.3.cloned.1.call-done = bf16[32,16,128]{2,1,0:T(8,128)(2,1)} async-done(((bf16[128,16,128]{2,1,0:T(8,128)(2,1)}), bf16[32,16,128]{2,1,0:T(8,128)(2,1)}) %reduce-scatter.3.cloned.1.call-update) | async-done | bytes 131088 | tf_op jit(solution)/shard_map/reduce_scatter | solution.py:39
  105.7 68.2 %reduce-scatter.5.cloned.1.call-done = bf16[32,16,128]{2,1,0:T(8,128)(2,1)} async-done(((bf16[256,16,128]{2,1,0:T(8,128)(2,1)}), bf16[32,16,128]{2,1,0:T(8,128)(2,1)}) %reduce-scatter.5.cloned.1.call-update) | async-done | bytes 131088 | tf_op jit(solution)/shard_map/reduce_scatter | solution.py:48
  (10 shorter events, 0.0 us)
Async XLA Ops:
  7.2 45.6 %all-gather.2.cloned.1.call-start = ((), (), s32[]{:S(2)}) async-start(), calls=%async_computation.3 | async-start | bytes 1179648 | tf_op jit(solution)/shard_map/all_gather | solution.py:18
  9.6 50.3 %copy-start.5 = (s32[128,256]{1,0:T(8,128)S(1)}, s32[128,256]{1,0:T(8,128)}, u32[]{:S(2)}) copy-start(s32[128,256]{1,0:T(8,128)} %param.7) | copy-start | bytes 393220
  9.6 50.3 %copy-start.4 = (bf16[16,128,256]{2,1,0:T(8,128)(2,1)S(1)}, bf16[16,128,256]{2,1,0:T(8,128)(2,1)}, u32[]{:S(2)}) copy-start(bf16[16,128,256]{2,1,0:T(8,128)(2,1)} %param.8) | copy-start | bytes 3145732
  55.6 22.3 %all-to-all-start = ((bf16[256,16,128]{2,1,0:T(8,128)(2,1)}), bf16[256,16,128]{2,1,0:T(8,128)(2,1)}, u32[]{:S(2)}, u32[]{:S(2)}) async-start(bf16[256,16,128]{2,1,0:T(8,128)(2,1)} %copy.19), calls=%async_computation | async-start | bytes 2097152 | tf_op jit(solution)/shard_map/all_to_all | solution.py:19
  59.9 45.8 %reduce-scatter.3.cloned.1.call-start = ((), (), s32[]{:S(2)}) async-start(), calls=%async_computation.4 | async-start | bytes 655360 | tf_op jit(solution)/shard_map/reduce_scatter | solution.py:39
  63.4 4.0 %copy-start.3 = (bf16[32,16,128]{2,0,1:T(8,128)(2,1)S(1)}, bf16[32,16,128]{2,0,1:T(8,128)(2,1)}, u32[]{:S(2)}) copy-start(bf16[32,16,128]{2,0,1:T(8,128)(2,1)} %copy_multiply_fusion) | copy-start | bytes 393220
  79.9 1.6 copy-start
  82.4 1.3 copy-start.1
  85.7 1.6 copy-start.2
  85.8 88.1 %reduce-scatter.5.cloned.1.call-start = ((), (), s32[]{:S(2)}) async-start(), calls=%async_computation.5 | async-start | bytes 1179648 | tf_op jit(solution)/shard_map/reduce_scatter | solution.py:48
Sparse Core Ops, SparseCore 0:
  10.6 42.1 all-gather.1
  85.9 19.7 reduce-scatter.2
  109.7 64.1 reduce-scatter.4
where the time goes:
time: 181 us; the launch traced here: 180 us
  waiting for transfers between devices  125 us (69%)
  local copies, waits for them, and re-layouts  17.4 us (10%)
  between operations  13.9 us (8%)
  blocking collectives  10.5 us (6%)
  other arithmetic  5.54 us (3%)
  starting transfers between devices  4.37 us (2%)
  matrix products  3.59 us (2%)
    reduce_scatter x1, waiting for transfers between devices, per_device(): lax.psum_scatter(jnp.einsum('cfij,cifk->jfk', residual_part, row_stack, p...  68.2 us
    all_gather x1, waiting for transfers between devices, per_device(): strided = lax.all_gather(flagged, 'row', axis=0, tiled=True)  43.1 us
    reduce_scatter x1, waiting for transfers between devices, per_device(): lax.psum_scatter(jnp.einsum('cfij,cjfk->ifk', residual_part, col_stack, p...  13.8 us
    all_gather x1, blocking collectives, per_device(): first_side = lax.all_gather(flagged, 'col', axis=0, tiled=True)  10.5 us
    unnamed x13, local copies, waits for them, and re-layouts  7.28 us
    all_to_all x1, starting transfers between devices, per_device(): lax.all_to_all(strided, 'col', split_axis=0, concat_axis=0, tiled=True)  4.24 us
  transfers between devices with their start and end apart: 4, of which 3 were waited for; matrix products, arithmetic and copies ran while one was open for 7% of the time, Pallas kernels for 0%

commit v1 on v0

v1 whole, which is shorter than its diff:
```python
import functools

import jax
import jax.numpy as jnp
from jax import lax
from jax.experimental import pallas as pl
from jax.experimental.pallas import tpu as pltpu
from jax.sharding import PartitionSpec as P

MESH = pl.DeviceIdType.MESH
GROUP = 2


def plain(fn):
    return fn()


def kernel(
    n_row, n_col, chunks, group,
    own, mask, w_hbm, obs_hbm, out_first, out_second,
    v1, v2, w_v, obs_v, gf, gf_sum, rc, rx, gs, gs_sum, ry, rz,
    in_sem, own_sem, xs, xr, ds, dr, zs, zr, ys, yr,
    cs, cr, ps, pr, hs, hr, qs, qr,
):
    ratio = n_row // n_col
    n_z = n_row // ratio
    n_x = n_col // 2
    row, col = lax.axis_index("row"), lax.axis_index("col")
    z, y = row // ratio, row % ratio
    x, core = col // 2, col % 2
    shard = own.shape[1]
    first_rows = n_col * shard
    second_rows = ratio * first_rows
    half = own.shape[2] // 2

    def col_at(step):
        return ((x + step) % n_x) * 2 + core

    partner = x * 2 + (1 - core)

    def row_y(step):
        return z * ratio + (y + step) % ratio

    def row_z(step):
        return ((z + step) % n_z) * ratio + y

    def span(k):
        return pl.ds(k * group, group)

    def remote(src, dst, ssem, rsem, to_row, to_col):
        return pltpu.make_async_remote_copy(
            src_ref=src, dst_ref=dst, send_sem=ssem, recv_sem=rsem,
            device_id=(to_row, to_col), device_id_type=MESH,
        )

    def send_x(k, d):
        return remote(own.at[span(k)], v1.at[span(k), col], xs.at[d - 1, k], xr.at[d - 1, k], row, col_at(d))

    def send_d(k, d):
        if d == 0:
            return remote(own.at[span(k)], v1.at[span(k), col], ds.at[0, k], dr.at[0, k], row, partner)
        piece = v1.at[span(k), col_at(n_x - d)]
        return remote(piece, piece, ds.at[d, k], dr.at[d, k], row, partner)

    def send_z(k, up, src):
        to = (z + 1 if up else z - 1) * ratio + y
        return remote(src, v2.at[span(k), y], zs.at[0 if up else 1, k], zr.at[k], to, col)

    def send_y(k, d, src):
        return remote(src, v2.at[span(k), y], ys.at[d - 1, k], yr.at[d - 1, k], row_y(d), col)

    def send_c(k):
        return remote(gf.at[span(k), :, 1 - core], rc.at[span(k)], cs.at[k], cr.at[k], row, partner)

    def send_p(k, d):
        return remote(gf_sum.at[span(k), (x + d) % n_x], rx.at[d - 1, span(k)], ps.at[d - 1, k], pr.at[d - 1, k], row, col_at(d))

    def send_h(k, d):
        return remote(gs.at[span(k), :, (y + d) % ratio], ry.at[d - 1, span(k)], hs.at[d - 1, k], hr.at[d - 1, k], row_y(d), col)

    def send_q(k, d):
        return remote(gs_sum.at[span(k), (z + d) % n_z], rz.at[d - 1, span(k)], qs.at[d - 1, k], qr.at[d - 1, k], row_z(d), col)

    home = z == col
    up_ok = jnp.logical_and(z >= col, z + 1 < n_z)
    down_ok = jnp.logical_and(z <= col, z >= 1)

    load_w = pltpu.make_async_copy(w_hbm, w_v, in_sem.at[0])
    load_obs = pltpu.make_async_copy(obs_hbm, obs_v, in_sem.at[1])
    load_own = pltpu.make_async_copy(own, v1.at[:, col], own_sem)
    load_w.start()
    load_obs.start()
    load_own.start()

    barrier = pltpu.get_barrier_semaphore()
    peers = [(row, partner)]
    peers += [(row, col_at(d)) for d in range(1, n_x)]
    peers += [(row_y(d), col) for d in range(1, ratio)]
    peers += [(row_z(d), col) for d in range(1, n_z)]
    for peer in peers:
        pl.semaphore_signal(barrier, inc=1, device_id=peer, device_id_type=MESH)
    pl.semaphore_wait(barrier, len(peers))

    @pl.loop(0, chunks)
    def _(k):
        for d in range(1, n_x):
            send_x(k, d).start()
        send_d(k, 0).start()

    load_own.wait()

    def forward(k, src):
        @pl.when(up_ok)
        def _():
            send_z(k, True, src).start()

        @pl.when(down_ok)
        def _():
            send_z(k, False, src).start()

        for d in range(1, ratio):
            send_y(k, d, src).start()

    @pl.loop(0, chunks + 1)
    def _(it):
        @pl.when(it < chunks)
        def _():
            for d in range(1, n_x):
                send_x(it, d).wait_recv()
                send_d(it, d).start()

        @pl.when(it >= 1)
        def _():
            k = it - 1
            for d in range(n_x):
                send_d(k, d).wait_recv()

            @pl.when(home)
            def _():
                forward(k, v1.at[span(k)])
                pltpu.make_async_copy(v1.at[span(k)], v2.at[span(k), y], zr.at[k]).start()

    load_w.wait()
    load_obs.wait()

    lane = lax.broadcasted_iota(jnp.int32, (1, 2 * half), 1)
    low_plus = jnp.where(lane < half, 1.0, -1.0).astype(jnp.float32)

    def compute(f):
        a = v1[f].astype(jnp.float32).reshape(first_rows, 2 * half)
        b = v2[f].astype(jnp.float32).reshape(second_rows, 2 * half).astype(jnp.bfloat16)
        turned = pltpu.roll(a, half, 1) * low_plus
        w = jnp.concatenate([a, turned], axis=0).astype(jnp.bfloat16)
        cross = lax.dot_general(w, b, (((1,), (1,)), ((), ())), preferred_element_type=jnp.float32)
        scale = mask[...].astype(jnp.float32) * w_v[f].astype(jnp.float32)
        res = jnp.concatenate(
            [
                (scale * (cross[:first_rows] - obs_v[0, f].astype(jnp.float32))).astype(jnp.bfloat16),
                (scale * (cross[first_rows:] - obs_v[1, f].astype(jnp.float32))).astype(jnp.bfloat16),
            ],
            axis=0,
        )
        t = jnp.dot(res, b, preferred_element_type=jnp.float32)
        g1 = t[:first_rows] - pltpu.roll(t[first_rows:], half, 1) * low_plus
        gf[f] = g1.reshape(n_x, 2, shard, 2 * half).astype(jnp.bfloat16)
        g2 = lax.dot_general(res, w, (((0,), (0,)), ((), ())), preferred_element_type=jnp.float32)
        gs[f] = g2.reshape(n_z, ratio, shard, 2 * half).astype(jnp.bfloat16)

    lag_y, lag_h, lag_c = 1, 3, 4

    @pl.loop(0, chunks + lag_c)
    def _(it):
        @pl.when(it < chunks)
        def _():
            pltpu.make_async_copy(v1.at[span(it)], v2.at[span(it), y], zr.at[it]).wait()

            @pl.when(jnp.logical_not(home))
            def _():
                forward(it, v2.at[span(it), y])

        @pl.when(jnp.logical_and(it >= lag_y, it < chunks + lag_y))
        def _():
            k = it - lag_y
            for d in range(1, ratio):
                send_y(k, d, v2.at[span(k), y]).wait_recv()
            for i in range(group):
                compute(k * group + i)
            send_c(k).start()
            for d in range(1, ratio):
                send_h(k, d).start()

        @pl.when(jnp.logical_and(it >= lag_h, it < chunks + lag_h))
        def _():
            k = it - lag_h
            for d in range(1, ratio):
                send_h(k, d).wait_recv()
            total = gs[span(k), :, y].astype(jnp.float32)
            for d in range(1, ratio):
                total = total + ry[d - 1, span(k)].astype(jnp.float32)
            gs_sum[span(k)] = total.astype(jnp.bfloat16)
            for d in range(1, n_z):
                send_q(k, d).start()

        @pl.when(it >= lag_c)
        def _():
            k = it - lag_c
            send_c(k).wait_recv()
            total = gf[span(k), :, core].astype(jnp.float32) + rc[span(k)].astype(jnp.float32)
            gf_sum[span(k)] = total.astype(jnp.bfloat16)
            for d in range(1, n_x):
                send_p(k, d).start()

    @pl.loop(0, chunks)
    def _(k):
        for d in range(1, n_x):
            send_p(k, d).wait_recv()
        total = gf_sum[span(k), x].astype(jnp.float32)
        for d in range(1, n_x):
            total = total + rx[d - 1, span(k)].astype(jnp.float32)
        out_first[span(k)] = total.astype(jnp.bfloat16)
        for d in range(1, n_z):
            send_q(k, d).wait_recv()
        total = gs_sum[span(k), z].astype(jnp.float32)
        for d in range(1, n_z):
            total = total + rz[d - 1, span(k)].astype(jnp.float32)
        out_second[span(k)] = total.astype(jnp.bfloat16)

    @pl.loop(0, chunks)
    def _(k):
        for d in range(1, n_x):
            send_x(k, d).wait_send()
            send_p(k, d).wait_send()
        for d in range(n_x):
            send_d(k, d).wait_send()
        src = v1.at[span(k)]

        @pl.when(up_ok)
        def _():
            send_z(k, True, src).wait_send()

        @pl.when(down_ok)
        def _():
            send_z(k, False, src).wait_send()

        for d in range(1, ratio):
            send_y(k, d, src).wait_send()
            send_h(k, d).wait_send()
        send_c(k).wait_send()
        for d in range(1, n_z):
            send_q(k, d).wait_send()


def per_device(n_row, n_col, spectra, window_flags, pair_mask, misfit_weight, observed):
    shard, freqs, width = spectra.shape
    ratio = n_row // n_col
    n_z, n_x = n_row // ratio, n_col // 2
    group = GROUP if freqs % GROUP == 0 else 1
    chunks = freqs // group
    flag_value = window_flags.astype(jnp.bfloat16)
    flag_both = jnp.concatenate([flag_value, flag_value], axis=1)
    own = jnp.transpose(spectra * flag_both[:, None, :], (1, 0, 2))
    bf = jnp.bfloat16
    vm = lambda *shape: pltpu.VMEM(shape, bf)
    dma = lambda *shape: pltpu.SemaphoreType.DMA(shape)
    first, second = pl.pallas_call(
        functools.partial(kernel, n_row, n_col, chunks, group),
        out_shape=[jax.ShapeDtypeStruct((freqs, shard, width), bf)] * 2,
        in_specs=[
            pl.BlockSpec(memory_space=pltpu.VMEM),
            pl.BlockSpec(memory_space=pltpu.VMEM),
            pl.BlockSpec(memory_space=pl.ANY),
            pl.BlockSpec(memory_space=pl.ANY),
        ],
        out_specs=[pl.BlockSpec(memory_space=pltpu.VMEM)] * 2,
        scratch_shapes=[
            vm(freqs, n_col, shard, width),
            vm(freqs, ratio, n_col, shard, width),
            pltpu.VMEM(misfit_weight.shape, bf),
            pltpu.VMEM(observed.shape, bf),
            vm(freqs, n_x, 2, shard, width),
            vm(freqs, n_x, shard, width),
            vm(freqs, n_x, shard, width),
            vm(n_x - 1, freqs, shard, width),
            vm(freqs, n_z, ratio, shard, width),
            vm(freqs, n_z, shard, width),
            vm(ratio - 1, freqs, n_z, shard, width),
            vm(n_z - 1, freqs, shard, width),
            dma(2), pltpu.SemaphoreType.DMA,
            dma(n_x - 1, chunks), dma(n_x - 1, chunks),
            dma(n_x, chunks), dma(n_x, chunks),
            dma(2, chunks), dma(chunks),
            dma(ratio - 1, chunks), dma(ratio - 1, chunks),
            dma(chunks), dma(chunks),
            dma(n_x - 1, chunks), dma(n_x - 1, chunks),
            dma(ratio - 1, chunks), dma(ratio - 1, chunks),
            dma(n_z - 1, chunks), dma(n_z - 1, chunks),
        ],
        compiler_params=pltpu.CompilerParams(collective_id=0, has_side_effects=True),
        name="adjoint",
    )(own, pair_mask, misfit_weight, observed)
    return jnp.transpose(first, (1, 0, 2)), jnp.transpose(second, (1, 0, 2))[None]


def solution(mesh):
    placed = (
        P(("row", "col"), None, None),
        P(("row", "col"), None),
        P("row", "col"),
        P(None, "row", "col"),
        P(None, None, "row", "col"),
    )
    return jax.shard_map(
        functools.partial(per_device, mesh.shape["row"], mesh.shape["col"]),
        mesh=mesh,
        in_specs=placed,
        out_specs=(P(("row", "col"), None, None), P("col", "row", None, None)),
        check_vma=False,
    )
```

time: 181 us -> 59.5 us (0.33)
  waiting for transfers between devices: 125 us -> 0 us
  Pallas kernels: 0 us -> 53 us
  local copies, waits for them, and re-layouts: 17.4 us -> 3.22 us
  between operations: 13.9 us -> 0.64 us
  blocking collectives: 10.5 us -> 0 us
  starting transfers between devices: 4.37 us -> 0 us
  matrix products: 3.59 us -> 0 us
  other arithmetic: 5.54 us -> 2.39 us
    reduce_scatter x2 -> x0, waiting for transfers between devices: 82.1 us -> none  [the longest x1 68.2 us: per_device(): lax.psum_scatter(jnp.einsum('cfij,cifk->jfk', residual_part, row_stack, p...]
    pallas_call x0 -> x1, Pallas kernels: none -> 53 us  [per_device(): pl.pallas_call(functools.partial(kernel, n_row, n_col, chunks, group), ou...]
    all_gather x1 -> x0, waiting for transfers between devices: 43.1 us -> none  [per_device(): strided = lax.all_gather(flagged, 'row', axis=0, tiled=True)]
    all_gather x1 -> x0, blocking collectives: 10.5 us -> none  [per_device(): first_side = lax.all_gather(flagged, 'col', axis=0, tiled=True)]
    all_to_all x1 -> x0, starting transfers between devices: 4.24 us -> none  [per_device(): lax.all_to_all(strided, 'col', split_axis=0, concat_axis=0, tiled=True)]
    unnamed x13 -> x2, local copies, waits for them, and re-layouts: 7.28 us -> 3.22 us
    convert_element_type x2 -> x0, local copies, waits for them, and re-layouts: 3.83 us -> none  [the longest x1 2.63 us: per_device(): grad_second = lax.psum_scatter(jnp.einsum('cfij,cifk->jfk', residual_part...]
    dot_general x3 -> x0, matrix products: 3.59 us -> none  [the longest x1 1.85 us: per_device(): jnp.einsum('cfij,cifk->jfk', residual_part, row_stack, preferred_element_...]
  transfers between devices with their start and end apart: 4 -> 0, of which waited for: 3 -> 0; matrix products, arithmetic and copies ran while one was open for 7% -> 0% of each run, Pallas kernels for 0% -> 0%
where the time goes in v1:
time: 59.5 us; the launch traced here: 59.2 us
  Pallas kernels  53 us (89%)
  local copies, waits for them, and re-layouts  3.22 us (5%)
  other arithmetic  2.39 us (4%)
  between operations  0.64 us (1%)
    pallas_call x1, Pallas kernels, per_device(): pl.pallas_call(functools.partial(kernel, n_row, n_col, chunks, group), ou...  53 us
    unnamed x2, local copies, waits for them, and re-layouts  3.22 us
    transpose x1, other arithmetic, per_device(): own = jnp.transpose(spectra * flag_both[:, None, :], (1, 0, 2))  1.59 us

profile of v1, /device:TPU:0, one launch (start us, length us, event | category | flops | bytes accessed | tf_op | source)
XLA Modules:
  0.0 59.2 jit_solution(16222871821957984925)
XLA Ops:
  0.6 0.7 %convert_element_type.3 = bf16[32,64]{1,0:T(8,128)(2,1)S(1)} convert(s32[32,64]{1,0:T(8,128)} %param.6) | non-fusion elementwise | flops 2048 | bytes 12288 | tf_op jit(solution)/shard_map/convert_element_type | solution.py:259
  1.4 0.1 pad_maximum_fusion
  1.4 1.6 %fusion.own = bf16[16,32,128]{2,1,0:T(8,128)(2,1)} fusion(bf16[32,16,128]{2,1,0:T(8,128)(2,1)} %param.5, bf16[32,128]{1,0:T(8,128)(2,1)S(1)} %pad_maximum_fusion), kind=kLoop, calls=%fused_computation.1 | loop fusion | flops 65536 | bytes 270336 | tf_op jit(solution)/shard_map/transpose | solution.py:261
  3.0 53.0 %adjoint.1 = (bf16[16,32,128]{2,1,0:T(8,128)(2,1)}, bf16[16,32,128]{2,1,0:T(8,128)(2,1)}) custom-call(bf16[16,32,128]{2,1,0:T(8,128)(2,1)} %fusion.own, s32[128,256]{1,0:T(8,128)} %mask.1, bf16[16,128,256]{2,1,0:T(8,128)(2,1)} %w_hbm.1, bf16[2,16,128,256]{3,2,1,0:T(8,128)(2,1)} %obs_hbm.1), custom_call_target="tpu_custom_call" | custom-call | tf_op jit(solution)/shard_map/adjoint/pallas_call | solution.py:265
  56.0 1.6 %copy.8 = bf16[32,16,128]{2,1,0:T(8,128)(2,1)} copy(bf16[32,16,128]{2,0,1:T(8,128)(2,1)} %bitcast.7) | data formatting | bytes 262144
  57.6 1.6 %copy.9 = bf16[1,32,16,128]{3,2,1,0:T(8,128)(2,1)} copy(bf16[1,32,16,128]{3,1,2,0:T(8,128)(2,1)} %bitcast.6) | data formatting | bytes 262144

commit v2 on v1

--- a/solution.py
+++ b/solution.py
@@ -11,15 +11,11 @@
 GROUP = 2
 
 
-def plain(fn):
-    return fn()
-
-
 def kernel(
     n_row, n_col, chunks, group,
     own, mask, w_hbm, obs_hbm, out_first, out_second,
     v1, v2, w_v, obs_v, gf, gf_sum, rc, rx, gs, gs_sum, ry, rz,
-    in_sem, own_sem, xs, xr, ds, dr, zs, zr, ys, yr,
+    in_sem, own_sem, fs, fr, zs, zr, lz, ys, yr,
     cs, cr, ps, pr, hs, hr, qs, qr,
 ):
     ratio = n_row // n_col
@@ -53,18 +49,11 @@
             device_id=(to_row, to_col), device_id_type=MESH,
         )
 
-    def send_x(k, d):
-        return remote(own.at[span(k)], v1.at[span(k), col], xs.at[d - 1, k], xr.at[d - 1, k], row, col_at(d))
-
-    def send_d(k, d):
-        if d == 0:
-            return remote(own.at[span(k)], v1.at[span(k), col], ds.at[0, k], dr.at[0, k], row, partner)
-        piece = v1.at[span(k), col_at(n_x - d)]
-        return remote(piece, piece, ds.at[d, k], dr.at[d, k], row, partner)
-
-    def send_z(k, up, src):
-        to = (z + 1 if up else z - 1) * ratio + y
-        return remote(src, v2.at[span(k), y], zs.at[0 if up else 1, k], zr.at[k], to, col)
+    def send_f(k, d):
+        return remote(own.at[span(k)], v1.at[span(k), col], fs.at[d - 1, k], fr.at[d - 1, k], row, (col + d) % n_col)
+
+    def send_z(k, d):
+        return remote(own.at[span(k)], v2.at[span(k), y, col], zs.at[d - 1, k], zr.at[col, k], row_z(d), z)
 
     def send_y(k, d, src):
         return remote(src, v2.at[span(k), y], ys.at[d - 1, k], yr.at[d - 1, k], row_y(d), col)
@@ -82,8 +71,6 @@
         return remote(gs_sum.at[span(k), (z + d) % n_z], rz.at[d - 1, span(k)], qs.at[d - 1, k], qr.at[d - 1, k], row_z(d), col)
 
     home = z == col
-    up_ok = jnp.logical_and(z >= col, z + 1 < n_z)
-    down_ok = jnp.logical_and(z <= col, z >= 1)
 
     load_w = pltpu.make_async_copy(w_hbm, w_v, in_sem.at[0])
     load_obs = pltpu.make_async_copy(obs_hbm, obs_v, in_sem.at[1])
@@ -93,52 +80,38 @@
     load_own.start()
 
     barrier = pltpu.get_barrier_semaphore()
-    peers = [(row, partner)]
-    peers += [(row, col_at(d)) for d in range(1, n_x)]
-    peers += [(row_y(d), col) for d in range(1, ratio)]
-    peers += [(row_z(d), col) for d in range(1, n_z)]
-    for peer in peers:
-        pl.semaphore_signal(barrier, inc=1, device_id=peer, device_id_type=MESH)
-    pl.semaphore_wait(barrier, len(peers))
+
+    def tell(to_row, to_col):
+        pl.semaphore_signal(barrier, inc=1, device_id=(to_row, to_col), device_id_type=MESH)
+
+    @pl.when(jnp.logical_not(home))
+    def _():
+        for j in range(n_col):
+            tell(col * ratio + y, j)
+
+    for d in range(1, n_z):
+        tell(row_z(d), col)
+    for d in range(1, ratio):
+        tell(row_y(d), col)
+    for d in range(1, n_col):
+        tell(row, (col + d) % n_col)
+    pl.semaphore_wait(barrier, n_col - 1 + 2 * (n_z - 1) + ratio - 1)
 
     @pl.loop(0, chunks)
     def _(k):
-        for d in range(1, n_x):
-            send_x(k, d).start()
-        send_d(k, 0).start()
+        for d in range(1, n_z):
+            send_z(k, d).start()
+        for d in range(1, n_col):
+            send_f(k, d).start()
 
     load_own.wait()
 
-    def forward(k, src):
-        @pl.when(up_ok)
-        def _():
-            send_z(k, True, src).start()
-
-        @pl.when(down_ok)
-        def _():
-            send_z(k, False, src).start()
-
-        for d in range(1, ratio):
-            send_y(k, d, src).start()
-
-    @pl.loop(0, chunks + 1)
-    def _(it):
-        @pl.when(it < chunks)
-        def _():
-            for d in range(1, n_x):
-                send_x(it, d).wait_recv()
-                send_d(it, d).start()
-
-        @pl.when(it >= 1)
-        def _():
-            k = it - 1
-            for d in range(n_x):
-                send_d(k, d).wait_recv()
-
-            @pl.when(home)
-            def _():
-                forward(k, v1.at[span(k)])
-                pltpu.make_async_copy(v1.at[span(k)], v2.at[span(k), y], zr.at[k]).start()
+    def wait_first(k):
+        for d in range(1, n_col):
+            send_f(k, d).wait_recv()
+
+    def local_copy(k):
+        return pltpu.make_async_copy(v1.at[span(k)], v2.at[span(k), y], lz.at[k])
 
     load_w.wait()
     load_obs.wait()
@@ -166,23 +139,40 @@
         g2 = lax.dot_general(res, w, (((0,), (0,)), ((), ())), preferred_element_type=jnp.float32)
         gs[f] = g2.reshape(n_z, ratio, shard, 2 * half).astype(jnp.bfloat16)
 
-    lag_y, lag_h, lag_c = 1, 3, 4
+    lag_y, lag_h, lag_c = 2, 4, 5
 
     @pl.loop(0, chunks + lag_c)
     def _(it):
         @pl.when(it < chunks)
         def _():
-            pltpu.make_async_copy(v1.at[span(it)], v2.at[span(it), y], zr.at[it]).wait()
+            @pl.when(home)
+            def _():
+                wait_first(it)
+                for d in range(1, ratio):
+                    send_y(it, d, v1.at[span(it)]).start()
+                local_copy(it).start()
 
             @pl.when(jnp.logical_not(home))
             def _():
-                forward(it, v2.at[span(it), y])
+                for j in range(n_col):
+                    remote(own.at[span(it)], v2.at[span(it), y, j], zs.at[0, it], zr.at[j, it], row, col).wait_recv()
+                for d in range(1, ratio):
+                    send_y(it, d, v2.at[span(it), y]).start()
 
         @pl.when(jnp.logical_and(it >= lag_y, it < chunks + lag_y))
         def _():
             k = it - lag_y
             for d in range(1, ratio):
                 send_y(k, d, v2.at[span(k), y]).wait_recv()
+
+            @pl.when(home)
+            def _():
+                local_copy(k).wait()
+
+            @pl.when(jnp.logical_not(home))
+            def _():
+                wait_first(k)
+
             for i in range(group):
                 compute(k * group + i)
             send_c(k).start()
@@ -228,25 +218,15 @@
     @pl.loop(0, chunks)
     def _(k):
         for d in range(1, n_x):
-            send_x(k, d).wait_send()
             send_p(k, d).wait_send()
-        for d in range(n_x):
-            send_d(k, d).wait_send()
-        src = v1.at[span(k)]
-
-        @pl.when(up_ok)
-        def _():
-            send_z(k, True, src).wait_send()
-
-        @pl.when(down_ok)
-        def _():
-            send_z(k, False, src).wait_send()
-
+        for d in range(1, n_col):
+            send_f(k, d).wait_send()
         for d in range(1, ratio):
-            send_y(k, d, src).wait_send()
+            send_y(k, d, v1.at[span(k)]).wait_send()
             send_h(k, d).wait_send()
         send_c(k).wait_send()
         for d in range(1, n_z):
+            send_z(k, d).wait_send()
             send_q(k, d).wait_send()
 
 
@@ -286,9 +266,8 @@
             vm(ratio - 1, freqs, n_z, shard, width),
             vm(n_z - 1, freqs, shard, width),
             dma(2), pltpu.SemaphoreType.DMA,
-            dma(n_x - 1, chunks), dma(n_x - 1, chunks),
-            dma(n_x, chunks), dma(n_x, chunks),
-            dma(2, chunks), dma(chunks),
+            dma(n_col - 1, chunks), dma(n_col - 1, chunks),
+            dma(n_z - 1, chunks), dma(n_col, chunks), dma(chunks),
             dma(ratio - 1, chunks), dma(ratio - 1, chunks),
             dma(chunks), dma(chunks),
             dma(n_x - 1, chunks), dma(n_x - 1, chunks),

time: 59.5 us -> 49.4 us (0.83)
  Pallas kernels: 53 us -> 42.9 us
    pallas_call x1, Pallas kernels: 53 us -> 42.9 us  [per_device(): pl.pallas_call(functools.partial(kernel, n_row, n_col, chunks, group), ou...]
where the time goes in v2:
time: 49.4 us; the launch traced here: 49.1 us
  Pallas kernels  42.9 us (87%)
  local copies, waits for them, and re-layouts  3.22 us (7%)
  other arithmetic  2.39 us (5%)
  between operations  0.64 us (1%)
    pallas_call x1, Pallas kernels, per_device(): pl.pallas_call(functools.partial(kernel, n_row, n_col, chunks, group), ou...  42.9 us
    unnamed x2, local copies, waits for them, and re-layouts  3.22 us
    transpose x1, other arithmetic, per_device(): own = jnp.transpose(spectra * flag_both[:, None, :], (1, 0, 2))  1.59 us

profile of v2, /device:TPU:0, one launch (start us, length us, event | category | flops | bytes accessed | tf_op | source)
XLA Modules:
  0.0 49.1 jit_solution(12670112200969411198)
XLA Ops:
  0.6 0.7 %convert_element_type.3 = bf16[32,64]{1,0:T(8,128)(2,1)S(1)} convert(s32[32,64]{1,0:T(8,128)} %param.6) | non-fusion elementwise | flops 2048 | bytes 12288 | tf_op jit(solution)/shard_map/convert_element_type | solution.py:239
  1.4 0.1 pad_maximum_fusion
  1.4 1.6 %fusion.own = bf16[16,32,128]{2,1,0:T(8,128)(2,1)} fusion(bf16[32,16,128]{2,1,0:T(8,128)(2,1)} %param.5, bf16[32,128]{1,0:T(8,128)(2,1)S(1)} %pad_maximum_fusion), kind=kLoop, calls=%fused_computation.1 | loop fusion | flops 65536 | bytes 270336 | tf_op jit(solution)/shard_map/transpose | solution.py:241
  3.0 42.9 %adjoint.1 = (bf16[16,32,128]{2,1,0:T(8,128)(2,1)}, bf16[16,32,128]{2,1,0:T(8,128)(2,1)}) custom-call(bf16[16,32,128]{2,1,0:T(8,128)(2,1)} %fusion.own, s32[128,256]{1,0:T(8,128)} %mask.1, bf16[16,128,256]{2,1,0:T(8,128)(2,1)} %w_hbm.1, bf16[2,16,128,256]{3,2,1,0:T(8,128)(2,1)} %obs_hbm.1), custom_call_target="tpu_custom_call" | custom-call | tf_op jit(solution)/shard_map/adjoint/pallas_call | solution.py:245
  45.9 1.6 %copy.8 = bf16[32,16,128]{2,1,0:T(8,128)(2,1)} copy(bf16[32,16,128]{2,0,1:T(8,128)(2,1)} %bitcast.7) | data formatting | bytes 262144
  47.5 1.6 %copy.9 = bf16[1,32,16,128]{3,2,1,0:T(8,128)(2,1)} copy(bf16[1,32,16,128]{3,1,2,0:T(8,128)(2,1)} %bitcast.6) | data formatting | bytes 262144

commit v3 on v2

--- a/solution.py
+++ b/solution.py
@@ -13,7 +13,8 @@
 
 def kernel(
     n_row, n_col, chunks, group,
-    own, mask, w_hbm, obs_hbm, out_first, out_second,
+    raw, flags, mask, w_hbm, obs_hbm, out_first, out_second,
+    own,
     v1, v2, w_v, obs_v, gf, gf_sum, rc, rx, gs, gs_sum, ry, rz,
     in_sem, own_sem, fs, fr, zs, zr, lz, ys, yr,
     cs, cr, ps, pr, hs, hr, qs, qr,
@@ -77,7 +78,6 @@
     load_own = pltpu.make_async_copy(own, v1.at[:, col], own_sem)
     load_w.start()
     load_obs.start()
-    load_own.start()
 
     barrier = pltpu.get_barrier_semaphore()
 
@@ -95,6 +95,12 @@
         tell(row_y(d), col)
     for d in range(1, n_col):
         tell(row, (col + d) % n_col)
+
+    flag_value = flags[...].astype(jnp.float32)
+    flag_both = jnp.concatenate([flag_value, flag_value], axis=1)
+    flagged = raw[...].astype(jnp.float32) * flag_both[:, None, :]
+    own[...] = jnp.transpose(flagged, (1, 0, 2)).astype(jnp.bfloat16)
+    load_own.start()
     pl.semaphore_wait(barrier, n_col - 1 + 2 * (n_z - 1) + ratio - 1)
 
     @pl.loop(0, chunks)
@@ -230,15 +236,17 @@
             send_q(k, d).wait_send()
 
 
+def turn_kernel(first, second, out_first, out_second):
+    for src, dst in ((first, out_first), (second, out_second)):
+        dst[...] = jnp.transpose(src[...].astype(jnp.float32), (1, 0, 2)).astype(jnp.bfloat16)
+
+
 def per_device(n_row, n_col, spectra, window_flags, pair_mask, misfit_weight, observed):
     shard, freqs, width = spectra.shape
     ratio = n_row // n_col
     n_z, n_x = n_row // ratio, n_col // 2
     group = GROUP if freqs % GROUP == 0 else 1
     chunks = freqs // group
-    flag_value = window_flags.astype(jnp.bfloat16)
-    flag_both = jnp.concatenate([flag_value, flag_value], axis=1)
-    own = jnp.transpose(spectra * flag_both[:, None, :], (1, 0, 2))
     bf = jnp.bfloat16
     vm = lambda *shape: pltpu.VMEM(shape, bf)
     dma = lambda *shape: pltpu.SemaphoreType.DMA(shape)
@@ -248,11 +256,13 @@
         in_specs=[
             pl.BlockSpec(memory_space=pltpu.VMEM),
             pl.BlockSpec(memory_space=pltpu.VMEM),
+            pl.BlockSpec(memory_space=pltpu.VMEM),
             pl.BlockSpec(memory_space=pl.ANY),
             pl.BlockSpec(memory_space=pl.ANY),
         ],
         out_specs=[pl.BlockSpec(memory_space=pltpu.VMEM)] * 2,
         scratch_shapes=[
+            vm(freqs, shard, width),
             vm(freqs, n_col, shard, width),
             vm(freqs, ratio, n_col, shard, width),
             pltpu.VMEM(misfit_weight.shape, bf),
@@ -276,8 +286,15 @@
         ],
         compiler_params=pltpu.CompilerParams(collective_id=0, has_side_effects=True),
         name="adjoint",
-    )(own, pair_mask, misfit_weight, observed)
-    return jnp.transpose(first, (1, 0, 2)), jnp.transpose(second, (1, 0, 2))[None]
+    )(spectra, window_flags, pair_mask, misfit_weight, observed)
+    first, second = pl.pallas_call(
+        turn_kernel,
+        out_shape=[jax.ShapeDtypeStruct((shard, freqs, width), bf)] * 2,
+        in_specs=[pl.BlockSpec(memory_space=pltpu.VMEM)] * 2,
+        out_specs=[pl.BlockSpec(memory_space=pltpu.VMEM)] * 2,
+        name="turn",
+    )(first, second)
+    return first, second[None]
 
 
 def solution(mesh):

time: 49.4 us -> 45.4 us (0.919)
  local copies, waits for them, and re-layouts: 3.22 us -> 0 us
  other arithmetic: 2.39 us -> 0 us
  Pallas kernels: 42.9 us -> 44.6 us
    unnamed x2 -> x0, local copies, waits for them, and re-layouts: 3.22 us -> none
    pallas_call x0 -> x1, Pallas kernels: none -> 1.74 us  [per_device(): pl.pallas_call(turn_kernel, out_shape=[jax.ShapeDtypeStruct((shard, freqs...]
    transpose x1 -> x0, other arithmetic: 1.59 us -> none  [per_device(): own = jnp.transpose(spectra * flag_both[:, None, :], (1, 0, 2))]
    convert_element_type x1 -> x0, other arithmetic: 0.72 us -> none  [per_device(): flag_value = window_flags.astype(jnp.bfloat16)]
where the time goes in v3:
time: 45.4 us; the launch traced here: 45.3 us
  Pallas kernels  44.6 us (98%)
  between operations  0.64 us (1%)
    pallas_call x1, Pallas kernels, per_device(): pl.pallas_call(functools.partial(kernel, n_row, n_col, chunks, group), ou...  42.9 us
    pallas_call x1, Pallas kernels, per_device(): pl.pallas_call(turn_kernel, out_shape=[jax.ShapeDtypeStruct((shard, freqs...  1.74 us

profile of v3, /device:TPU:0, one launch (start us, length us, event | category | flops | bytes accessed | tf_op | source)
XLA Modules:
  0.0 45.3 jit_solution(6677917673496730095)
XLA Ops:
  0.6 42.9 %adjoint.1 = (bf16[16,32,128]{2,1,0:T(8,128)(2,1)}, bf16[16,32,128]{2,1,0:T(8,128)(2,1)}) custom-call(bf16[32,16,128]{2,1,0:T(8,128)(2,1)} %raw.1, s32[32,64]{1,0:T(8,128)} %flags.1, s32[128,256]{1,0:T(8,128)} %mask.1, bf16[16,128,256]{2,1,0:T(8,128)(2,1)} %w_hbm.1, bf16[2,16,128,256]{3,2,1,0:T(8,128)(2,1)} %obs_hbm.1), custom_call_target="tpu_custom_call" | custom-call | tf_op jit(solution)/shard_map/adjoint/pallas_call | solution.py:253
  43.5 1.7 %turn.1 = (bf16[32,16,128]{2,1,0:T(8,128)(2,1)}, bf16[32,16,128]{2,1,0:T(8,128)(2,1)}) custom-call(bf16[16,32,128]{2,1,0:T(8,128)(2,1)} %get-tuple-element.6.first, bf16[16,32,128]{2,1,0:T(8,128)(2,1)} %get-tuple-element.7.second), custom_call_target="tpu_custom_call" | custom-call | tf_op jit(solution)/shard_map/turn/pallas_call | solution.py:290

commit v4 on v3

--- a/solution.py
+++ b/solution.py
@@ -9,19 +9,21 @@
 
 MESH = pl.DeviceIdType.MESH
 GROUP = 2
+LAG_Y, LAG_B, LAG_C = 2, 3, 5
 
 
 def kernel(
     n_row, n_col, chunks, group,
-    raw, flags, mask, w_hbm, obs_hbm, out_first, out_second,
-    own,
-    v1, v2, w_v, obs_v, gf, gf_sum, rc, rx, gs, gs_sum, ry, rz,
+    raw_hbm, flags_hbm, mask_hbm, w_hbm, obs_hbm, out_first, out_second,
+    raw, flags, mask, own,
+    v1, v2, w_v, obs_v, gf, gf_sum, rc, rx, sums, halves, last, ry,
     in_sem, own_sem, fs, fr, zs, zr, lz, ys, yr,
-    cs, cr, ps, pr, hs, hr, qs, qr,
+    cs, cr, ps, pr, hs, hr, bs, br,
 ):
     ratio = n_row // n_col
     n_z = n_row // ratio
     n_x = n_col // 2
+    bits = n_z.bit_length() - 1
     row, col = lax.axis_index("row"), lax.axis_index("col")
     z, y = row // ratio, row % ratio
     x, core = col // 2, col % 2
@@ -51,33 +53,42 @@
         )
 
     def send_f(k, d):
-        return remote(own.at[span(k)], v1.at[span(k), col], fs.at[d - 1, k], fr.at[d - 1, k], row, (col + d) % n_col)
+        return remote(own.at[span(k)], v1.at[span(k), col], fs.at[d - 1], fr.at[k], row, (col + d) % n_col)
 
     def send_z(k, d):
-        return remote(own.at[span(k)], v2.at[span(k), y, col], zs.at[d - 1, k], zr.at[col, k], row_z(d), z)
+        return remote(own.at[span(k)], v2.at[span(k), y, col], zs.at[d - 1], zr.at[k], row_z(d), z)
 
     def send_y(k, d, src):
-        return remote(src, v2.at[span(k), y], ys.at[d - 1, k], yr.at[d - 1, k], row_y(d), col)
+        return remote(src, v2.at[span(k), y], ys.at[d - 1], yr.at[d - 1, k], row_y(d), col)
 
     def send_c(k):
-        return remote(gf.at[span(k), :, 1 - core], rc.at[span(k)], cs.at[k], cr.at[k], row, partner)
+        return remote(gf.at[span(k), :, 1 - core], rc.at[span(k)], cs, cr.at[k], row, partner)
 
     def send_p(k, d):
-        return remote(gf_sum.at[span(k), (x + d) % n_x], rx.at[d - 1, span(k)], ps.at[d - 1, k], pr.at[d - 1, k], row, col_at(d))
+        return remote(gf_sum.at[span(k), (x + d) % n_x], rx.at[d - 1, span(k)], ps.at[d - 1], pr.at[d - 1, k], row, col_at(d))
+
+    def bit(b):
+        return (z // 2**b) % 2
+
+    def row_bit(b):
+        return (z + (1 - 2 * bit(b)) * 2**b) * ratio + y
+
+    def send_b(k, b):
+        return remote(sums[b].at[span(k), :, 1 - bit(b)], halves[b].at[span(k)], bs.at[b], br.at[b, k], row_bit(b), col)
 
     def send_h(k, d):
-        return remote(gs.at[span(k), :, (y + d) % ratio], ry.at[d - 1, span(k)], hs.at[d - 1, k], hr.at[d - 1, k], row_y(d), col)
-
-    def send_q(k, d):
-        return remote(gs_sum.at[span(k), (z + d) % n_z], rz.at[d - 1, span(k)], qs.at[d - 1, k], qr.at[d - 1, k], row_z(d), col)
+        return remote(last.at[span(k), (y + d) % ratio], ry.at[d - 1, span(k)], hs.at[d - 1], hr.at[d - 1, k], row_y(d), col)
 
     home = z == col
 
     load_w = pltpu.make_async_copy(w_hbm, w_v, in_sem.at[0])
     load_obs = pltpu.make_async_copy(obs_hbm, obs_v, in_sem.at[1])
     load_own = pltpu.make_async_copy(own, v1.at[:, col], own_sem)
-    load_w.start()
-    load_obs.start()
+    load_raw = pltpu.make_async_copy(raw_hbm, raw, in_sem.at[2])
+    load_flags = pltpu.make_async_copy(flags_hbm, flags, in_sem.at[3])
+    load_mask = pltpu.make_async_copy(mask_hbm, mask, in_sem.at[4])
+    load_raw.start()
+    load_flags.start()
 
     barrier = pltpu.get_barrier_semaphore()
 
@@ -89,19 +100,24 @@
         for j in range(n_col):
             tell(col * ratio + y, j)
 
-    for d in range(1, n_z):
-        tell(row_z(d), col)
+    for b in range(bits):
+        tell(row_bit(b), col)
     for d in range(1, ratio):
         tell(row_y(d), col)
     for d in range(1, n_col):
         tell(row, (col + d) % n_col)
 
+    load_raw.wait()
+    load_flags.wait()
+    load_mask.start()
+    load_w.start()
+    load_obs.start()
     flag_value = flags[...].astype(jnp.float32)
     flag_both = jnp.concatenate([flag_value, flag_value], axis=1)
     flagged = raw[...].astype(jnp.float32) * flag_both[:, None, :]
     own[...] = jnp.transpose(flagged, (1, 0, 2)).astype(jnp.bfloat16)
     load_own.start()
-    pl.semaphore_wait(barrier, n_col - 1 + 2 * (n_z - 1) + ratio - 1)
+    pl.semaphore_wait(barrier, n_col - 1 + n_z - 1 + bits + ratio - 1)
 
     @pl.loop(0, chunks)
     def _(k):
@@ -113,12 +129,13 @@
     load_own.wait()
 
     def wait_first(k):
-        for d in range(1, n_col):
-            send_f(k, d).wait_recv()
+        got = v1.at[span(k), pl.ds(0, n_col - 1)]
+        pltpu.make_async_copy(got, got, fr.at[k]).wait()
 
     def local_copy(k):
         return pltpu.make_async_copy(v1.at[span(k)], v2.at[span(k), y], lz.at[k])
 
+    load_mask.wait()
     load_w.wait()
     load_obs.wait()
 
@@ -143,11 +160,12 @@
         g1 = t[:first_rows] - pltpu.roll(t[first_rows:], half, 1) * low_plus
         gf[f] = g1.reshape(n_x, 2, shard, 2 * half).astype(jnp.bfloat16)
         g2 = lax.dot_general(res, w, (((0,), (0,)), ((), ())), preferred_element_type=jnp.float32)
-        gs[f] = g2.reshape(n_z, ratio, shard, 2 * half).astype(jnp.bfloat16)
-
-    lag_y, lag_h, lag_c = 2, 4, 5
-
-    @pl.loop(0, chunks + lag_c)
+        sums[0][f] = g2.reshape(n_z // 2, 2, ratio, shard, 2 * half).astype(jnp.bfloat16)
+
+    lag_y, lag_c = LAG_Y, LAG_C
+    lag_b = [lag_y + LAG_B * (b + 1) for b in range(bits)]
+
+    @pl.loop(0, chunks + max(lag_b[-1], lag_c))
     def _(it):
         @pl.when(it < chunks)
         def _():
@@ -160,8 +178,8 @@
 
             @pl.when(jnp.logical_not(home))
             def _():
-                for j in range(n_col):
-                    remote(own.at[span(it)], v2.at[span(it), y, j], zs.at[0, it], zr.at[j, it], row, col).wait_recv()
+                got = v2.at[span(it), y]
+                pltpu.make_async_copy(got, got, zr.at[it]).wait()
                 for d in range(1, ratio):
                     send_y(it, d, v2.at[span(it), y]).start()
 
@@ -182,22 +200,25 @@
             for i in range(group):
                 compute(k * group + i)
             send_c(k).start()
-            for d in range(1, ratio):
-                send_h(k, d).start()
-
-        @pl.when(jnp.logical_and(it >= lag_h, it < chunks + lag_h))
-        def _():
-            k = it - lag_h
-            for d in range(1, ratio):
-                send_h(k, d).wait_recv()
-            total = gs[span(k), :, y].astype(jnp.float32)
-            for d in range(1, ratio):
-                total = total + ry[d - 1, span(k)].astype(jnp.float32)
-            gs_sum[span(k)] = total.astype(jnp.bfloat16)
-            for d in range(1, n_z):
-                send_q(k, d).start()
-
-        @pl.when(it >= lag_c)
+            send_b(k, 0).start()
+
+        for b in range(bits):
+            @pl.when(jnp.logical_and(it >= lag_b[b], it < chunks + lag_b[b]))
+            def _():
+                k = it - lag_b[b]
+                send_b(k, b).wait_recv()
+                total = sums[b][span(k), :, bit(b)].astype(jnp.float32) + halves[b][span(k)].astype(jnp.float32)
+                if b + 1 < bits:
+                    sums[b + 1][span(k)] = total.reshape(
+                        group, n_z // 2 ** (b + 2), 2, ratio, shard, 2 * half
+                    ).astype(jnp.bfloat16)
+                    send_b(k, b + 1).start()
+                else:
+                    last[span(k)] = total[:, 0].astype(jnp.bfloat16)
+                    for d in range(1, ratio):
+                        send_h(k, d).start()
+
+        @pl.when(jnp.logical_and(it >= lag_c, it < chunks + lag_c))
         def _():
             k = it - lag_c
             send_c(k).wait_recv()
@@ -214,26 +235,27 @@
         for d in range(1, n_x):
             total = total + rx[d - 1, span(k)].astype(jnp.float32)
         out_first[span(k)] = total.astype(jnp.bfloat16)
-        for d in range(1, n_z):
-            send_q(k, d).wait_recv()
-        total = gs_sum[span(k), z].astype(jnp.float32)
-        for d in range(1, n_z):
-            total = total + rz[d - 1, span(k)].astype(jnp.float32)
+        total = last[span(k), y].astype(jnp.float32)
+        for d in range(1, ratio):
+            send_h(k, d).wait_recv()
+            total = total + ry[d - 1, span(k)].astype(jnp.float32)
         out_second[span(k)] = total.astype(jnp.bfloat16)
 
-    @pl.loop(0, chunks)
-    def _(k):
-        for d in range(1, n_x):
-            send_p(k, d).wait_send()
-        for d in range(1, n_col):
-            send_f(k, d).wait_send()
-        for d in range(1, ratio):
-            send_y(k, d, v1.at[span(k)]).wait_send()
-            send_h(k, d).wait_send()
-        send_c(k).wait_send()
-        for d in range(1, n_z):
-            send_z(k, d).wait_send()
-            send_q(k, d).wait_send()
+    def sent(ref, sem):
+        pltpu.make_async_copy(ref, ref, sem).wait()
+
+    for d in range(1, n_col):
+        sent(own, fs.at[d - 1])
+    for d in range(1, n_z):
+        sent(own, zs.at[d - 1])
+    for d in range(1, ratio):
+        sent(v1, ys.at[d - 1])
+        sent(own, hs.at[d - 1])
+    for d in range(1, n_x):
+        sent(own, ps.at[d - 1])
+    sent(rc, cs)
+    for b in range(bits):
+        sent(halves[b], bs.at[b])
 
 
 def turn_kernel(first, second, out_first, out_second):
@@ -245,6 +267,7 @@
     shard, freqs, width = spectra.shape
     ratio = n_row // n_col
     n_z, n_x = n_row // ratio, n_col // 2
+    bits = n_z.bit_length() - 1
     group = GROUP if freqs % GROUP == 0 else 1
     chunks = freqs // group
     bf = jnp.bfloat16
@@ -254,14 +277,13 @@
         functools.partial(kernel, n_row, n_col, chunks, group),
         out_shape=[jax.ShapeDtypeStruct((freqs, shard, width), bf)] * 2,
         in_specs=[
-            pl.BlockSpec(memory_space=pltpu.VMEM),
-            pl.BlockSpec(memory_space=pltpu.VMEM),
-            pl.BlockSpec(memory_space=pltpu.VMEM),
             pl.BlockSpec(memory_space=pl.ANY),
-            pl.BlockSpec(memory_space=pl.ANY),
-        ],
+        ] * 5,
         out_specs=[pl.BlockSpec(memory_space=pltpu.VMEM)] * 2,
         scratch_shapes=[
+            pltpu.VMEM(spectra.shape, bf),
+            pltpu.VMEM(window_flags.shape, window_flags.dtype),
+            pltpu.VMEM(pair_mask.shape, pair_mask.dtype),
             vm(freqs, shard, width),
             vm(freqs, n_col, shard, width),
             vm(freqs, ratio, n_col, shard, width),
@@ -271,18 +293,18 @@
             vm(freqs, n_x, shard, width),
             vm(freqs, n_x, shard, width),
             vm(n_x - 1, freqs, shard, width),
-            vm(freqs, n_z, ratio, shard, width),
-            vm(freqs, n_z, shard, width),
-            vm(ratio - 1, freqs, n_z, shard, width),
-            vm(n_z - 1, freqs, shard, width),
-            dma(2), pltpu.SemaphoreType.DMA,
-            dma(n_col - 1, chunks), dma(n_col - 1, chunks),
-            dma(n_z - 1, chunks), dma(n_col, chunks), dma(chunks),
-            dma(ratio - 1, chunks), dma(ratio - 1, chunks),
-            dma(chunks), dma(chunks),
-            dma(n_x - 1, chunks), dma(n_x - 1, chunks),
-            dma(ratio - 1, chunks), dma(ratio - 1, chunks),
-            dma(n_z - 1, chunks), dma(n_z - 1, chunks),
+            [vm(freqs, n_z // 2 ** (b + 1), 2, ratio, shard, width) for b in range(bits)],
+            [vm(freqs, n_z // 2 ** (b + 1), ratio, shard, width) for b in range(bits)],
+            vm(freqs, ratio, shard, width),
+            vm(ratio - 1, freqs, shard, width),
+            dma(5), pltpu.SemaphoreType.DMA,
+            dma(n_col - 1), dma(chunks),
+            dma(n_z - 1), dma(chunks), dma(chunks),
+            dma(ratio - 1), dma(ratio - 1, chunks),
+            pltpu.SemaphoreType.DMA, dma(chunks),
+            dma(n_x - 1), dma(n_x - 1, chunks),
+            dma(ratio - 1), dma(ratio - 1, chunks),
+            dma(bits), dma(bits, chunks),
         ],
         compiler_params=pltpu.CompilerParams(collective_id=0, has_side_effects=True),
         name="adjoint",

time: 45.4 us -> 41.9 us (0.923)
  Pallas kernels: 44.6 us -> 41.1 us
    pallas_call x1, Pallas kernels: 42.9 us -> 39.4 us  [per_device(): pl.pallas_call(functools.partial(kernel, n_row, n_col, chunks, group), ou...]
where the time goes in v4:
time: 41.9 us; the launch traced here: 41.8 us
  Pallas kernels  41.1 us (98%)
  between operations  0.64 us (2%)
    pallas_call x1, Pallas kernels, per_device(): pl.pallas_call(functools.partial(kernel, n_row, n_col, chunks, group), ou...  39.4 us
    pallas_call x1, Pallas kernels, per_device(): pl.pallas_call(turn_kernel, out_shape=[jax.ShapeDtypeStruct((shard, freqs...  1.74 us

profile of v4, /device:TPU:0, one launch (start us, length us, event | category | flops | bytes accessed | tf_op | source)
XLA Modules:
  0.0 41.8 jit_solution(7317354591331097267)
XLA Ops:
  0.6 39.4 %adjoint.1 = (bf16[16,32,128]{2,1,0:T(8,128)(2,1)}, bf16[16,32,128]{2,1,0:T(8,128)(2,1)}) custom-call(bf16[32,16,128]{2,1,0:T(8,128)(2,1)} %raw_hbm.1, s32[32,64]{1,0:T(8,128)} %flags_hbm.1, s32[128,256]{1,0:T(8,128)} %mask_hbm.1, bf16[16,128,256]{2,1,0:T(8,128)(2,1)} %w_hbm.1, bf16[2,16,128,256]{3,2,1,0:T(8,128)(2,1)} %obs_hbm.1), custom_call_target="tpu_custom_call" | custom-call | tf_op jit(solution)/shard_map/adjoint/pallas_call | solution.py:276
  40.0 1.7 %turn.1 = (bf16[32,16,128]{2,1,0:T(8,128)(2,1)}, bf16[32,16,128]{2,1,0:T(8,128)(2,1)}) custom-call(bf16[16,32,128]{2,1,0:T(8,128)(2,1)} %get-tuple-element.6.first, bf16[16,32,128]{2,1,0:T(8,128)(2,1)} %get-tuple-element.7.second), custom_call_target="tpu_custom_call" | custom-call | tf_op jit(solution)/shard_map/turn/pallas_call | solution.py:312

commit v5 on v4

--- a/solution.py
+++ b/solution.py
@@ -9,7 +9,7 @@
 
 MESH = pl.DeviceIdType.MESH
 GROUP = 2
-LAG_Y, LAG_B, LAG_C = 2, 3, 5
+LAG_Y, LAG_B, LAG_C = 3, 3, 7
 
 
 def kernel(
@@ -121,7 +121,7 @@
 
     @pl.loop(0, chunks)
     def _(k):
-        for d in range(1, n_z):
+        for d in range(n_z - 1, 0, -1):
             send_z(k, d).start()
         for d in range(1, n_col):
             send_f(k, d).start()
@@ -134,10 +134,6 @@
 
     def local_copy(k):
         return pltpu.make_async_copy(v1.at[span(k)], v2.at[span(k), y], lz.at[k])
-
-    load_mask.wait()
-    load_w.wait()
-    load_obs.wait()
 
     lane = lax.broadcasted_iota(jnp.int32, (1, 2 * half), 1)
     low_plus = jnp.where(lane < half, 1.0, -1.0).astype(jnp.float32)
@@ -186,6 +182,13 @@
         @pl.when(jnp.logical_and(it >= lag_y, it < chunks + lag_y))
         def _():
             k = it - lag_y
+
+            @pl.when(k == 0)
+            def _():
+                load_mask.wait()
+                load_w.wait()
+                load_obs.wait()
+
             for d in range(1, ratio):
                 send_y(k, d, v2.at[span(k), y]).wait_recv()
 
@@ -309,11 +312,13 @@
         compiler_params=pltpu.CompilerParams(collective_id=0, has_side_effects=True),
         name="adjoint",
     )(spectra, window_flags, pair_mask, misfit_weight, observed)
+    parts = 2 if shard % 32 == 0 else 1
     first, second = pl.pallas_call(
         turn_kernel,
         out_shape=[jax.ShapeDtypeStruct((shard, freqs, width), bf)] * 2,
-        in_specs=[pl.BlockSpec(memory_space=pltpu.VMEM)] * 2,
-        out_specs=[pl.BlockSpec(memory_space=pltpu.VMEM)] * 2,
+        grid=(parts,),
+        in_specs=[pl.BlockSpec((freqs, shard // parts, width), lambda i: (0, i, 0))] * 2,
+        out_specs=[pl.BlockSpec((shard // parts, freqs, width), lambda i: (i, 0, 0))] * 2,
         name="turn",
     )(first, second)
     return first, second[None]

time: 41.9 us -> 40.6 us (0.969)
  Pallas kernels: 41.1 us -> 39.7 us
    pallas_call x1, Pallas kernels: 39.4 us -> 38.1 us  [per_device(): pl.pallas_call(functools.partial(kernel, n_row, n_col, chunks, group), ou...]
where the time goes in v5:
time: 40.6 us; the launch traced here: 40.4 us
  Pallas kernels  39.7 us (98%)
  between operations  0.64 us (2%)
    pallas_call x1, Pallas kernels, per_device(): pl.pallas_call(functools.partial(kernel, n_row, n_col, chunks, group), ou...  38.1 us
    pallas_call x1, Pallas kernels, per_device(): pl.pallas_call(turn_kernel, out_shape=[jax.ShapeDtypeStruct((shard, freqs...  1.66 us

profile of v5, /device:TPU:0, one launch (start us, length us, event | category | flops | bytes accessed | tf_op | source)
XLA Modules:
  0.0 40.4 jit_solution(17316857738869250074)
XLA Ops:
  0.6 38.1 %adjoint.1 = (bf16[16,32,128]{2,1,0:T(8,128)(2,1)}, bf16[16,32,128]{2,1,0:T(8,128)(2,1)}) custom-call(bf16[32,16,128]{2,1,0:T(8,128)(2,1)} %raw_hbm.1, s32[32,64]{1,0:T(8,128)} %flags_hbm.1, s32[128,256]{1,0:T(8,128)} %mask_hbm.1, bf16[16,128,256]{2,1,0:T(8,128)(2,1)} %w_hbm.1, bf16[2,16,128,256]{3,2,1,0:T(8,128)(2,1)} %obs_hbm.1), custom_call_target="tpu_custom_call" | custom-call | tf_op jit(solution)/shard_map/adjoint/pallas_call | solution.py:279
  38.7 1.7 %turn.1 = (bf16[32,16,128]{2,1,0:T(8,128)(2,1)}, bf16[32,16,128]{2,1,0:T(8,128)(2,1)}) custom-call(bf16[16,32,128]{2,1,0:T(8,128)(2,1)} %get-tuple-element.6.first, bf16[16,32,128]{2,1,0:T(8,128)(2,1)} %get-tuple-element.7.second), custom_call_target="tpu_custom_call" | custom-call | tf_op jit(solution)/shard_map/turn/pallas_call | solution.py:316

commit v6 on v5

--- a/solution.py
+++ b/solution.py
@@ -202,8 +202,8 @@
 
             for i in range(group):
                 compute(k * group + i)
+            send_b(k, 0).start()
             send_c(k).start()
-            send_b(k, 0).start()
 
         for b in range(bits):
             @pl.when(jnp.logical_and(it >= lag_b[b], it < chunks + lag_b[b]))

time: 40.6 us -> 40.6 us (level)
  no operation moved by 1% of the time
where the time goes in v6:
time: 40.6 us; the launch traced here: 40.4 us
  Pallas kernels  39.7 us (98%)
  between operations  0.64 us (2%)
    pallas_call x1, Pallas kernels, per_device(): pl.pallas_call(functools.partial(kernel, n_row, n_col, chunks, group), ou...  38.1 us
    pallas_call x1, Pallas kernels, per_device(): pl.pallas_call(turn_kernel, out_shape=[jax.ShapeDtypeStruct((shard, freqs...  1.66 us

profile of v6, /device:TPU:0, one launch (start us, length us, event | category | flops | bytes accessed | tf_op | source)
XLA Modules:
  0.0 40.4 jit_solution(13451009489790780584)
XLA Ops:
  0.6 38.1 %adjoint.1 = (bf16[16,32,128]{2,1,0:T(8,128)(2,1)}, bf16[16,32,128]{2,1,0:T(8,128)(2,1)}) custom-call(bf16[32,16,128]{2,1,0:T(8,128)(2,1)} %raw_hbm.1, s32[32,64]{1,0:T(8,128)} %flags_hbm.1, s32[128,256]{1,0:T(8,128)} %mask_hbm.1, bf16[16,128,256]{2,1,0:T(8,128)(2,1)} %w_hbm.1, bf16[2,16,128,256]{3,2,1,0:T(8,128)(2,1)} %obs_hbm.1), custom_call_target="tpu_custom_call" | custom-call | tf_op jit(solution)/shard_map/adjoint/pallas_call | solution.py:279
  38.7 1.7 %turn.1 = (bf16[32,16,128]{2,1,0:T(8,128)(2,1)}, bf16[32,16,128]{2,1,0:T(8,128)(2,1)}) custom-call(bf16[16,32,128]{2,1,0:T(8,128)(2,1)} %get-tuple-element.6.first, bf16[16,32,128]{2,1,0:T(8,128)(2,1)} %get-tuple-element.7.second), custom_call_target="tpu_custom_call" | custom-call | tf_op jit(solution)/shard_map/turn/pallas_call | solution.py:316
